TPU v7x, 128 devices: a whole 4x4x4 slice. The times are simulated.
128 devices in a mesh: slab: 32 (over z, y, core), sub: 4 (over x).
Axes of the slice: x: 4, y: 4, z: 4, core: 2. Of those that a mesh axis runs over, the one named last changes fastest.
Arguments:
- factor_obs: float32 [128, 64, 64, 512], P('slab', 'sub'), may hold values from -0.1484375 to 0.1484375
- factor_ctrl: float32 [128, 64, 64, 512], P('slab', 'sub'), may hold values from -0.1484375 to 0.1484375
- diffusivity: float32 [128, 4096], P('slab', 'sub'), may hold values from 0.5 to 2
- input_map: float32 [4, 128, 4096], P(None, 'slab', 'sub'), may hold values from -1 to 1
- output_map: float32 [4, 128, 4096], P(None, 'slab', 'sub'), may hold values from -1 to 1
- start_block: float32 [512, 128], replicated, may hold values from -6 to 6
- order: int32 [1], replicated, may hold values from 64 to 128
Outputs:
- reduced_mass: float32 [128, 128], replicated
- reduced_state: float32 [128, 128], replicated
- reduced_input: float32 [128, 4], replicated
- reduced_output: float32 [4, 128], replicated
All inputs are finite; a program needn't handle non-finite values.
Results may differ from a plain program's by a relative error of at most 0.00017.
Values sent between devices are 32-bit elements; how exact they have to be, the bound alone decides.
A program may use at most 128 MiB of HBM per device.

v0:
```python
import jax
import jax.numpy as jnp
from jax import lax
from jax.experimental import pallas as pl
from jax.experimental.pallas import tpu as pltpu
from jax.sharding import Mesh
from jax.sharding import PartitionSpec as P

SLAB = ("slab_0", "slab_1", "slab_2")

MESH = pl.DeviceIdType.MESH
STEP = 16
FLOOR = 2e-4


def position():
    z, y, c, x = (lax.axis_index(n) for n in ("slab_0", "slab_1", "slab_2", "sub"))
    return z, y, c, x


def peer_near(d):
    z, y, c, x = position()
    return (z, lax.rem(y + d * c, 4), c, lax.rem(x + d * (1 - c), 4))


def peer_next(d):
    z, y, c, x = position()
    return (z, lax.rem(y + d * (1 - c), 4), c, lax.rem(x + d * c, 4))


def peer_far(d):
    z, y, c, x = position()
    return (lax.rem(z + d, 4), y, c, x)


def partner():
    z, y, c, x = position()
    return (z, y, 1 - c, x)


def meet():
    barrier = pltpu.get_barrier_semaphore()
    pl.semaphore_signal(barrier, inc=1, device_id=partner(), device_id_type=MESH)
    for peers in (peer_near, peer_next, peer_far):
        for d in (1, 2, 3):
            pl.semaphore_signal(barrier, inc=1, device_id=peers(d), device_id_type=MESH)
    pl.semaphore_wait(barrier, 10)


def remote(src, dst, send, recv, to):
    return pltpu.make_async_remote_copy(
        src_ref=src, dst_ref=dst, send_sem=send, recv_sem=recv, device_id=to, device_id_type=MESH
    )


def rows(start, count):
    return pl.ds(pl.multiple_of(start, 8), count)


def big_kernel(x_ref, o_ref, in_c, acc_c, in_1, acc_1, in_2, acc_2, in_z, send, recv):
    z, y, c, x = position()
    near = x * (1 - c) + y * c
    nxt = y * (1 - c) + x * c
    half = x_ref.shape[0] // 2
    quarter = half // 4
    piece = quarter // 4
    meet()
    copy = remote(x_ref.at[rows((1 - c) * half, half)], in_c, send.at[0], recv.at[0], partner())
    copy.start()
    copy.wait()
    acc_c[...] = x_ref[rows(c * half, half), :] + in_c[...]
    copies = []
    for d in (1, 2, 3):
        copies.append(
            remote(
                acc_c.at[rows(lax.rem(near + d, 4) * quarter, quarter)],
                in_1.at[d - 1], send.at[d], recv.at[d], peer_near(d),
            )
        )
        copies[-1].start()
    for copy in copies:
        copy.wait()
    acc_1[...] = (acc_c[rows(near * quarter, quarter), :] + in_1[0]) + (in_1[1] + in_1[2])
    copies = []
    for d in (1, 2, 3):
        copies.append(
            remote(
                acc_1.at[rows(lax.rem(nxt + d, 4) * piece, piece)],
                in_2.at[d - 1], send.at[3 + d], recv.at[3 + d], peer_next(d),
            )
        )
        copies[-1].start()
    for copy in copies:
        copy.wait()
    mine = (acc_1[rows(nxt * piece, piece), :] + in_2[0]) + (in_2[1] + in_2[2])
    acc_2[...] = mine
    copies = []
    for d in (1, 2, 3):
        copies.append(
            remote(acc_2, in_z.at[z], send.at[6 + d], recv.at[6 + d], peer_far(d))
        )
        copies[-1].start()
    in_z[z] = mine
    for copy in copies:
        copy.wait()
    low = c * half + near * quarter
    at = low + nxt * piece
    o_ref[rows(at, piece), :] = (in_z[0] + in_z[1]) + (in_z[2] + in_z[3])
    copies = []
    for d in (1, 2, 3):
        block = o_ref.at[rows(at, piece)]
        copies.append(remote(block, block, send.at[9 + d], recv.at[9 + d], peer_next(d)))
        copies[-1].start()
    for copy in copies:
        copy.wait()
    copies = []
    for d in (1, 2, 3):
        block = o_ref.at[rows(low, quarter)]
        copies.append(remote(block, block, send.at[12 + d], recv.at[12 + d], peer_near(d)))
        copies[-1].start()
    for copy in copies:
        copy.wait()
    block = o_ref.at[rows(c * half, half)]
    copy = remote(block, block, send.at[16], recv.at[16], partner())
    copy.start()
    copy.wait()


def total_big(value):
    n, w = value.shape
    f = jnp.float32
    vm = pl.BlockSpec(memory_space=pltpu.VMEM)
    return pl.pallas_call(
        big_kernel,
        out_shape=jax.ShapeDtypeStruct(value.shape, f),
        in_specs=[vm],
        out_specs=vm,
        scratch_shapes=[
            pltpu.VMEM((n // 2, w), f),
            pltpu.VMEM((n // 2, w), f),
            pltpu.VMEM((3, n // 8, w), f),
            pltpu.VMEM((n // 8, w), f),
            pltpu.VMEM((3, n // 32, w), f),
            pltpu.VMEM((n // 32, w), f),
            pltpu.VMEM((4, n // 32, w), f),
            pltpu.SemaphoreType.DMA((17,)),
            pltpu.SemaphoreType.DMA((17,)),
        ],
        compiler_params=pltpu.CompilerParams(collective_id=0, has_side_effects=True),
        name="total_big",
    )(value)


def small_kernel(x_ref, o_ref, in_c, acc, in_1, in_2, in_3, send, recv):
    z, y, c, x = position()
    near = x * (1 - c) + y * c
    nxt = y * (1 - c) + x * c
    half = x_ref.shape[0] // 2
    meet()
    copy = remote(x_ref.at[rows((1 - c) * half, half)], in_c, send.at[0], recv.at[0], partner())
    copy.start()
    copy.wait()
    value = x_ref[rows(c * half, half), :] + in_c[...]
    stages = ((in_1, near, peer_near, 1), (in_2, nxt, peer_next, 4), (in_3, z, peer_far, 7))
    for stage, (into, me, peers, first) in enumerate(stages):
        acc[stage] = value
        copies = []
        for d in (1, 2, 3):
            k = first + d - 1
            copies.append(remote(acc.at[stage], into.at[me], send.at[k], recv.at[k], peers(d)))
            copies[-1].start()
        into[me] = value
        for copy in copies:
            copy.wait()
        value = (into[0] + into[1]) + (into[2] + into[3])
    block = o_ref.at[rows(c * half, half)]
    o_ref[rows(c * half, half), :] = value
    copy = remote(block, block, send.at[10], recv.at[10], partner())
    copy.start()
    copy.wait()


def total_small(value):
    n, w = value.shape
    f = jnp.float32
    vm = pl.BlockSpec(memory_space=pltpu.VMEM)
    return pl.pallas_call(
        small_kernel,
        out_shape=jax.ShapeDtypeStruct(value.shape, f),
        in_specs=[vm],
        out_specs=vm,
        scratch_shapes=[
            pltpu.VMEM((n // 2, w), f),
            pltpu.VMEM((3, n // 2, w), f),
            pltpu.VMEM((4, n // 2, w), f),
            pltpu.VMEM((4, n // 2, w), f),
            pltpu.VMEM((4, n // 2, w), f),
            pltpu.SemaphoreType.DMA((11,)),
            pltpu.SemaphoreType.DMA((11,)),
        ],
        compiler_params=pltpu.CompilerParams(collective_id=1, has_side_effects=True),
        name="total_small",
    )(value)


def split(value):
    high = value.astype(jnp.bfloat16)
    return high, (value - high.astype(jnp.float32)).astype(jnp.bfloat16)


def mul(first, second, contract):
    return lax.dot_general(
        first, second, (((contract[0],), (contract[1],)), ((), ())),
        preferred_element_type=jnp.float32,
    )


def gram_kernel(o_ref, c_ref, out_ref):
    @pl.when(pl.program_id(0) == 0)
    def _():
        out_ref[...] = jnp.zeros_like(out_ref)

    o_high, o_low = split(o_ref[...])
    c_high, c_low = split(c_ref[...])
    out_ref[...] += (
        mul(o_high, c_high, (0, 0)) + mul(o_high, c_low, (0, 0)) + mul(o_low, c_high, (0, 0))
    )


def gram(observe, control, block=1024):
    cells, rank = observe.shape
    spec = pl.BlockSpec((block, rank), lambda k: (k, 0))
    return pl.pallas_call(
        gram_kernel,
        grid=(cells // block,),
        out_shape=jax.ShapeDtypeStruct((rank, rank), jnp.float32),
        in_specs=[spec, spec],
        out_specs=pl.BlockSpec((rank, rank), lambda k: (0, 0)),
        compiler_params=pltpu.CompilerParams(dimension_semantics=("arbitrary",)),
        name="gram",
    )(observe, control)


def product(first, second, contract):
    return lax.dot_general(
        first, second, (((contract[0],), (contract[1],)), ((), ())),
        precision=lax.Precision.HIGHEST, preferred_element_type=jnp.float32,
    )


def factor(pairs):
    n = pairs[0][0].shape[0]
    f = jnp.float32
    row = lax.broadcasted_iota(jnp.int32, (STEP, n), 0)
    least = None
    eye = (
        lax.broadcasted_iota(jnp.int32, (n, n), 0) == lax.broadcasted_iota(jnp.int32, (n, n), 1)
    ).astype(f)
    for a, b in pairs:
        b[...] = eye
    for first in range(0, n, STEP):
        here = slice(first, first + STEP)
        work = []
        for a, b in pairs:
            across = a[here, :]
            cols = [
                jnp.broadcast_to(across[:, first + j : first + j + 1], (STEP, n))
                for j in range(STEP)
            ]
            work.append([across, b[here, :], cols, jnp.ones((STEP, n), f)])
        for j in range(STEP):
            for item in work:
                across, inverse, cols, pivots = item
                pivot = jnp.broadcast_to(cols[j][j : j + 1, :], (STEP, n))
                item[3] = jnp.where(row == j, pivot, pivots)
                if j == STEP - 1:
                    continue
                ratio = jnp.where(row > j, cols[j] / pivot, 0.0)
                for i in range(j + 1, STEP):
                    cols[i] = cols[i] - ratio * cols[i][j : j + 1, :]
                item[0] = across - ratio * across[j : j + 1, :]
                item[1] = inverse - ratio * inverse[j : j + 1, :]
        for (a, b), (across, inverse, cols, pivots) in zip(pairs, work):
            diag = jnp.sum(
                jnp.where(
                    lax.broadcasted_iota(jnp.int32, (STEP, n), 1) == row + first, a[here, :], 0.0
                ),
                axis=1,
                keepdims=True,
            )
            share = jnp.min(pivots[:, :1] / diag)
            least = share if least is None else jnp.minimum(least, share)
            scale = lax.rsqrt(pivots)
            upper = across * scale
            lower = inverse * scale
            a[here, :] = jnp.where(
                lax.broadcasted_iota(jnp.int32, (STEP, n), 1) >= row + first, upper, 0.0
            )
            b[here, :] = lower
            if first + STEP < n:
                rest = slice(first + STEP, n)
                change = product(upper, jnp.concatenate([upper, lower], axis=1), (0, 0))
                a[rest, :] = a[rest, :] - change[rest, :n]
                b[rest, :] = b[rest, :] - change[rest, n:]
    return least


def unit_rows(value):
    return value * lax.rsqrt(jnp.sum(value * value, axis=1, keepdims=True))


def bases_kernel(order_ref, m_ref, s_ref, right_ref, left_ref, mass_ref, a3, b3, a4, b4, y3, y4):
    n = a3.shape[0]
    m = m_ref
    y1 = unit_rows(product(s_ref[...].T, m[...], (1, 0)))
    y2 = unit_rows(product(y1, m[...], (1, 1)))
    y3[...] = unit_rows(product(y2, m[...], (1, 0)))
    y4[...] = product(y3[...], m[...], (1, 1))
    a3[...] = product(y3[...], y3[...], (1, 1))
    a4[...] = product(y4[...], y4[...], (1, 1))
    least = factor(((a3, b3), (a4, b4)))

    y3[...] = product(b3[...], y3[...], (1, 0))
    y4[...] = product(b4[...], y4[...], (1, 0))
    mass_ref[...] = product(a4[...], b3[...], (1, 1))

    @pl.when(jnp.logical_not(least > FLOOR))
    def _():
        y3[...] = s_ref[...].T

        def sweep(step, _):
            y4[...] = product(y3[...], m[...], (1, 0))
            a3[...] = product(y4[...], y4[...], (1, 1))
            factor(((a3, b3),))
            y3[...] = product(b3[...], y4[...], (1, 0))
            y4[...] = product(y3[...], m[...], (1, 1))
            a3[...] = product(y4[...], y4[...], (1, 1))
            a4[...] = y4[:, :n]
            factor(((a3, b3),))
            left_ref[...] = product(b3[...], y4[...], (1, 0))
            right_ref[...] = y3[...]
            mass_ref[...] = product(left_ref[...], y4[...], (1, 1))
            y3[...] = left_ref[...]
            return 0

        lax.fori_loop(0, 2, sweep, 0)
        y3[...] = right_ref[...]
        y4[...] = left_ref[...]

    order = order_ref[0]
    down = (lax.broadcasted_iota(jnp.int32, (n, n), 0) < order).astype(jnp.float32)
    along = (lax.broadcasted_iota(jnp.int32, (n, n), 1) < order).astype(jnp.float32)
    right_ref[...] = y3[...] * down[:, :1]
    left_ref[...] = y4[...] * down[:, :1]
    mass_ref[...] = mass_ref[...] * down * along


def bases(cross_gram, start_block, order):
    rank, n = start_block.shape
    f = jnp.float32
    vm = pl.BlockSpec(memory_space=pltpu.VMEM)
    return pl.pallas_call(
        bases_kernel,
        out_shape=(
            jax.ShapeDtypeStruct((n, rank), f),
            jax.ShapeDtypeStruct((n, rank), f),
            jax.ShapeDtypeStruct((n, n), f),
        ),
        in_specs=[pl.BlockSpec(memory_space=pltpu.SMEM), vm, vm],
        out_specs=(vm, vm, vm),
        scratch_shapes=[pltpu.VMEM((n, n), f)] * 4 + [pltpu.VMEM((n, rank), f)] * 2,
        name="bases",
    )(order, cross_gram, start_block)

def padded_2(value, sides, width):
    edges = {}
    for axis, dim in sides:
        count, length = (lax.axis_size(axis), value.shape[dim])
        up = [(i, (i + 1) % count) for i in range(count - 1)]
        last = lax.slice_in_dim(value, length - width, length, axis=dim)
        initial = lax.slice_in_dim(value, 0, width, axis=dim)
        edges[dim] = (
            lax.ppermute(last, axis, up),
            lax.ppermute(initial, axis, [(b, a) for a, b in up]),
        )
    done = []
    for _, dim in sides:
        low, high = edges[dim]
        around = [(width, width) if d in done else (0, 0) for d in range(value.ndim)]
        value = jnp.concatenate([jnp.pad(low, around), value, jnp.pad(high, around)], axis=dim)
        done.append(dim)
    return value


def matmul(first, second, contract):
    return lax.dot_general(
        first, second, (((contract[0],), (contract[1],)), ((), ())),
        precision=lax.Precision.HIGH, preferred_element_type=jnp.float32,
    )


def stencil_padded(padded, conduct):
    center = padded[1:-1, 1:-1]
    beside = padded[2:, 1:-1] + padded[:-2, 1:-1] + padded[1:-1, 2:] + padded[1:-1, :-2]
    along = jnp.pad(center, ((0, 0), (0, 0), (1, 1), (0, 0)))
    beside = beside + along[:, :, 2:] + along[:, :, :-2]
    return conduct[..., None] * (beside - 6.0 * center) / 6.0


def on_device(factor_obs, factor_ctrl, diffusivity, input_map, output_map, start_block, order):
    plane_count, line_count, point_count, rank_count = factor_ctrl.shape
    cell_count = plane_count * line_count * point_count
    observe = factor_obs.reshape(cell_count, rank_count)
    control = factor_ctrl.reshape(cell_count, rank_count)
    conduct = diffusivity.reshape(plane_count, line_count, point_count)
    drive = input_map.reshape(input_map.shape[0], cell_count)
    sense = output_map.reshape(output_map.shape[0], cell_count)
    basis_count = start_block.shape[1]
    cross_gram = total_big(gram(observe, control))
    right, left, reduced_mass = bases(cross_gram, start_block, order)
    ctrl_space = matmul(control, right, (1, 1))
    padded = padded_2(
        ctrl_space.reshape(plane_count, line_count, point_count, basis_count),
        ((SLAB, 0), ("sub", 1)),
        1,
    )
    obs_space = matmul(observe, left, (1, 1))
    applied = stencil_padded(padded, conduct).reshape(cell_count, basis_count)
    parts = jnp.concatenate(
        [
            matmul(obs_space, applied, (0, 0)),
            matmul(drive, obs_space, (1, 0)),
            matmul(sense, ctrl_space, (1, 0)),
            jnp.zeros((8, basis_count), jnp.float32),
        ]
    )
    whole = total_small(parts)
    n = basis_count
    return (reduced_mass, whole[:n], whole[n : n + 4].T, whole[n + 4 : n + 8])


def solution(mesh):
    torus = Mesh(
        mesh.devices.reshape(4, 4, 2, mesh.shape["sub"]), ("slab_0", "slab_1", "slab_2", "sub")
    )
    placed = (
        P(SLAB, "sub", None, None),
        P(SLAB, "sub", None, None),
        P(SLAB, "sub"),
        P(None, SLAB, "sub"),
        P(None, SLAB, "sub"),
        P(),
        P(),
    )
    return jax.shard_map(
        on_device, mesh=torus, in_specs=placed, out_specs=(P(), P(), P(), P()), check_vma=False
    )
```

profile of v0, /device:TPU:1, one launch (start us, length us, event | category | flops | bytes accessed | tf_op | source)
XLA Modules:
  0.0 127.0 jit_solution(7650607666240469846)
XLA Ops:
  1.3 11.2 %gram.1.x_ref = f32[512,512]{1,0:T(8,128)} custom-call(f32[4096,512]{1,0:T(8,128)} %bitcast.29, f32[4096,512]{1,0:T(8,128)} %bitcast.27), custom_call_target="tpu_custom_call" | custom-call | tf_op jit(solution)/shard_map/gram/pallas_call | solution.py:233
  12.4 37.5 %total_big.1.m_ref = f32[512,512]{1,0:T(8,128)} custom-call(f32[512,512]{1,0:T(8,128)} %gram.1.x_ref), custom_call_target="tpu_custom_call" | custom-call | tf_op jit(solution)/shard_map/total_big/pallas_call | solution.py:133
  50.0 13.0 %bases.1 = (f32[128,512]{1,0:T(8,128)}, f32[128,512]{1,0:T(8,128)}, f32[128,128]{1,0:T(8,128)}) custom-call(s32[1]{0:T(128)S(6)} %copy.20.order_ref, f32[512,512]{1,0:T(8,128)} %total_big.1.m_ref, f32[512,128]{1,0:T(8,128)} %s_ref.1), custom_call_target="tpu_custom_call" | custom-call | tf_op jit(solution)/shard_map/bases/pallas_call | solution.py:362
  63.0 7.7 %fusion.14 = f32[128,4096]{1,0:T(8,128)S(1)} fusion(f32[128,512]{1,0:T(8,128)} %get-tuple-element.9, f32[4096,512]{1,0:T(8,128)} %bitcast.28), kind=kOutput, calls=%fused_computation.30 | convolution fusion | flops 1610612736 | bytes 10747904 | tf_op jit(solution)/shard_map/dot_general | solution.py:396
  70.7 1.8 %copy.15 = f32[4096,128]{1,0:T(8,128)} copy(f32[4096,128]{0,1:T(8,128)S(1)} %bitcast.31) | data formatting | bytes 4194304 | tf_op jit(solution)/shard_map/dot_general | solution.py:396
  72.5 1.7 %fusion.10 = (f32[4,1,64,128]{3,2,1,0:T(8,128)}, f32[4,1,64,128]{3,2,1,0:T(8,128)}) fusion(f32[4,16,64,128]{3,2,1,0:T(8,128)} %bitcast.33), kind=kLoop, calls=%fused_computation.26 | loop fusion | bytes 524288 | tf_op jit(solution)/shard_map/slice | solution.py:381
  74.2 0.0 copy-start.3
  74.2 1.7 %collective-permute-start.3 = (f32[4,1,64,128]{3,2,1,0:T(8,128)}, f32[4,1,64,128]{3,2,1,0:T(8,128)S(1)}, u32[]{:S(2)}, u32[]{:S(2)}) collective-permute-start(f32[4,1,64,128]{3,2,1,0:T(8,128)} %get-tuple-element.11), channel_id=1, source_target_pairs={{0,1},{1,2},{2,3},{4,5},{5,6},{6,7},{8,9},{9,10},{10,11},{12,13},{... | collective-permute-start | bytes 393224 | tf_op jit(solution)/shard_map/ppermute | solution.py:383
  75.9 0.1 fusion.11
  76.0 1.0 copy.16
  77.0 2.3 %collective-permute-start = (f32[1,16,64,128]{3,2,1,0:T(8,128)}, f32[1,16,64,128]{3,2,1,0:T(8,128)}, u32[]{:S(2)}, u32[]{:S(2)}) collective-permute-start(f32[1,16,64,128]{3,2,1,0:T(8,128)} %bitcast.36), channel_id=1, source_target_pairs={{4,0},{8,4},{12,8},{16,12},{20,16},{24,20},{28,24},{32,28},{36,32}... | collective-permute-start | bytes 1572872 | tf_op jit(solution)/shard_map/ppermute | solution.py:384
  79.4 0.2 copy.17
  79.5 3.2 %collective-permute-start.1 = (f32[1,16,64,128]{3,2,1,0:T(8,128)S(1)}, f32[1,16,64,128]{3,2,1,0:T(8,128)S(1)}, u32[]{:S(2)}, u32[]{:S(2)}) collective-permute-start(f32[1,16,64,128]{3,2,1,0:T(8,128)S(1)} %bitcast.37), channel_id=1, source_target_pairs={{0,4},{4,8},{8,12},{12,16},{16,20},{20,24},{24,28},{28,32},{32,36}... | collective-permute-start | bytes 1572872 | tf_op jit(solution)/shard_map/ppermute | solution.py:383
  82.8 1.3 %collective-permute-start.2 = (f32[4,1,64,128]{3,2,1,0:T(8,128)}, f32[4,1,64,128]{3,2,1,0:T(8,128)}, u32[]{:S(2)}, u32[]{:S(2)}) collective-permute-start(f32[4,1,64,128]{3,2,1,0:T(8,128)} %get-tuple-element.10), channel_id=1, source_target_pairs={{1,0},{2,1},{3,2},{5,4},{6,5},{7,6},{9,8},{10,9},{11,10},{13,12},{... | collective-permute-start | bytes 393224 | tf_op jit(solution)/shard_map/ppermute | solution.py:384
  84.1 0.9 copy.19
  85.0 0.0 copy-done.3
  85.0 0.0 copy-start.4
  85.0 7.6 %fusion.13 = f32[128,4096]{1,0:T(8,128)S(1)} fusion(f32[128,512]{1,0:T(8,128)S(1)} %copy-done.3, f32[4096,512]{1,0:T(8,128)} %bitcast.30), kind=kOutput, calls=%fused_computation.29 | convolution fusion | flops 1610612736 | bytes 10747904 | tf_op jit(solution)/shard_map/dot_general | solution.py:396
  92.7 0.0 copy-start
  92.7 0.0 copy-done.4
  92.7 0.0 copy-start.5
  92.7 0.9 convolution_bitcast_fusion
  93.7 0.0 copy-start.2
  93.7 0.3 copy-done
  94.0 0.9 convolution_bitcast_fusion.1
  94.9 0.0 copy-done.5
  94.9 0.1 mul.13
  95.0 0.1 pad.17.clone
  95.1 0.0 copy-start.1
  95.1 0.0 collective-permute-done.3
  95.1 0.0 collective-permute-done.2
  95.1 0.0 collective-permute-done
  95.1 0.0 collective-permute-done.1
  95.1 0.2 copy-done.2
  95.3 3.7 %fusion.4 = f32[4,16,64,128]{3,2,1,0:T(8,128)S(1)} fusion(f32[4,16,64,128]{3,2,1,0:T(8,128)S(1)} %bitcast.34, f32[4,1,64,128]{3,2,1,0:T(8,128)S(1)} %collective-permute-done.3, f32[1,16,64,128]{3,2,1,0:T(8,128)} %collective-permute-done, f32[1,16,64,128]{3,2,1,0:T(8,128)S(1)} %collective-permute-done.1, f32[4,1,64,128]{3,2,1,0:T(8,128)} %collective-permute-done.2, ...), kind=kLoop, calls=%fused_computation.6 | loop fusion | flops 12058624 | bytes 5521408 | tf_op jit(solution)/shard_map/div | solution.py:407
  99.0 0.0 copy-done.1
  99.0 1.3 %fusion.15 = f32[128,128]{1,0:T(8,128)S(1)} fusion(f32[128,4096]{1,0:T(8,128)S(1)} %copy-done.1, f32[4096,128]{1,0:T(8,128)S(1)} %bitcast.35), kind=kOutput, calls=%fused_computation.31 | convolution fusion | flops 402653184 | bytes 4259840 | tf_op jit(solution)/shard_map/dot_general | solution.py:396
  100.3 0.7 maximum_maximum_fusion.x_ref
  101.1 23.2 %total_small.1 = f32[144,128]{1,0:T(8,128)} custom-call(f32[144,128]{1,0:T(8,128)} %maximum_maximum_fusion.x_ref), custom_call_target="tpu_custom_call" | custom-call | tf_op jit(solution)/shard_map/total_small/pallas_call | solution.py:187
  124.2 1.5 %slice.61 = f32[128,128]{1,0:T(8,128)} slice(f32[144,128]{1,0:T(8,128)} %total_small.1), slice={[0:128], [0:128]} | slice | bytes 131072 | tf_op jit(solution)/shard_map/slice | solution.py:439
  125.7 1.3 %fusion.12 = (f32[4,128]{1,0:T(4,128)}, f32[128,4]{0,1:T(4,128)}) fusion(f32[144,128]{1,0:T(8,128)} %total_small.1), kind=kLoop, calls=%fused_computation.28 | loop fusion | bytes 8192 | tf_op jit(solution)/shard_map/slice | solution.py:439
  (2 shorter events, 0.0 us)
Async XLA Ops:
  74.2 10.8 %copy-start.3 = (f32[128,512]{1,0:T(8,128)S(1)}, f32[128,512]{1,0:T(8,128)}, u32[]{:S(2)}) copy-start(f32[128,512]{1,0:T(8,128)} %get-tuple-element.8) | copy-start | bytes 786436
  74.2 20.9 %collective-permute-start.3 = (f32[4,1,64,128]{3,2,1,0:T(8,128)}, f32[4,1,64,128]{3,2,1,0:T(8,128)S(1)}, u32[]{:S(2)}, u32[]{:S(2)}) collective-permute-start(f32[4,1,64,128]{3,2,1,0:T(8,128)} %get-tuple-element.11), channel_id=1, source_target_pairs={{0,1},{1,2},{2,3},{4,5},{5,6},{6,7},{8,9},{9,10},{10,11},{12,13},{... | collective-permute-start | bytes 393224 | tf_op jit(solution)/shard_map/ppermute | solution.py:383
  77.0 18.0 %collective-permute-start = (f32[1,16,64,128]{3,2,1,0:T(8,128)}, f32[1,16,64,128]{3,2,1,0:T(8,128)}, u32[]{:S(2)}, u32[]{:S(2)}) collective-permute-start(f32[1,16,64,128]{3,2,1,0:T(8,128)} %bitcast.36), channel_id=1, source_target_pairs={{4,0},{8,4},{12,8},{16,12},{20,16},{24,20},{28,24},{32,28},{36,32}... | collective-permute-start | bytes 1572872 | tf_op jit(solution)/shard_map/ppermute | solution.py:384
  79.5 15.5 %collective-permute-start.1 = (f32[1,16,64,128]{3,2,1,0:T(8,128)S(1)}, f32[1,16,64,128]{3,2,1,0:T(8,128)S(1)}, u32[]{:S(2)}, u32[]{:S(2)}) collective-permute-start(f32[1,16,64,128]{3,2,1,0:T(8,128)S(1)} %bitcast.37), channel_id=1, source_target_pairs={{0,4},{4,8},{8,12},{12,16},{16,20},{20,24},{24,28},{28,32},{32,36}... | collective-permute-start | bytes 1572872 | tf_op jit(solution)/shard_map/ppermute | solution.py:383
  82.8 12.3 %collective-permute-start.2 = (f32[4,1,64,128]{3,2,1,0:T(8,128)}, f32[4,1,64,128]{3,2,1,0:T(8,128)}, u32[]{:S(2)}, u32[]{:S(2)}) collective-permute-start(f32[4,1,64,128]{3,2,1,0:T(8,128)} %get-tuple-element.10), channel_id=1, source_target_pairs={{1,0},{2,1},{3,2},{5,4},{6,5},{7,6},{9,8},{10,9},{11,10},{13,12},{... | collective-permute-start | bytes 393224 | tf_op jit(solution)/shard_map/ppermute | solution.py:384
  85.0 7.7 %copy-start.4 = (f32[4,4,1024]{2,1,0:T(4,128)S(1)}, f32[4,4,1024]{2,1,0:T(4,128)}, u32[]{:S(2)}) copy-start(f32[4,4,1024]{2,1,0:T(4,128)} %param.10) | copy-start | bytes 196612
  92.7 1.3 %copy-start = (f32[128,4096]{1,0:T(8,128)}, f32[128,4096]{1,0:T(8,128)S(1)}, u32[]{:S(2)}) copy-start(f32[128,4096]{1,0:T(8,128)S(1)} %fusion.13) | copy-start | bytes 6291460
  92.7 2.2 %copy-start.5 = (f32[4,1024]{1,0:T(4,128)S(1)}, f32[4,1024]{1,0:T(4,128)}, u32[]{:S(2)}) copy-start(f32[4,1024]{1,0:T(4,128)} %param.9) | copy-start | bytes 49156
  93.7 1.6 %copy-start.2 = (f32[4096,128]{1,0:T(8,128)S(1)}, f32[4096,128]{1,0:T(8,128)}, u32[]{:S(2)}) copy-start(f32[4096,128]{1,0:T(8,128)} %copy.15) | copy-start | bytes 6291460
  95.1 4.0 %copy-start.1 = (f32[128,4096]{1,0:T(8,128)S(1)}, f32[128,4096]{1,0:T(8,128)}, u32[]{:S(2)}) copy-start(f32[128,4096]{1,0:T(8,128)} %copy-done) | copy-start | bytes 6291460
where the time goes:
time: 128 us; the launch traced here: 127 us
  Pallas kernels  84.8 us (66%)
  matrix products  18.5 us (14%)
  local copies, waits for them, and re-layouts  9.25 us (7%)
  starting transfers between devices  8.57 us (7%)
  other arithmetic  4.45 us (3%)
  between operations  1.46 us (1%)
    pallas_call x1, Pallas kernels, total_big(): pl.pallas_call(big_kernel, out_shape=jax.ShapeDtypeStruct(value.shape, f)...  37.5 us
    pallas_call x1, Pallas kernels, total_small(): pl.pallas_call(small_kernel, out_shape=jax.ShapeDtypeStruct(value.shape,...  23.2 us
    dot_general x5, matrix products, matmul(): lax.dot_general(first, second, (((contract[0],), (contract[1],)), ((), ()...  18.5 us
    pallas_call x1, Pallas kernels, bases(): pl.pallas_call(bases_kernel, out_shape=(jax.ShapeDtypeStruct((n, rank), f...  13 us
    pallas_call x1, Pallas kernels, gram(): pl.pallas_call(gram_kernel, grid=(cells // block,), out_shape=jax.ShapeDt...  11.2 us
    ppermute x2, starting transfers between devices, padded_2(): lax.ppermute(last, axis, up)  4.96 us
    div x1, other arithmetic, stencil_padded(): return conduct[..., None] * (beside - 6.0 * center) / 6.0  3.73 us
    ppermute x2, starting transfers between devices, padded_2(): lax.ppermute(initial, axis, [(b, a) for a, b in up])  3.6 us
  transfers between devices with their start and end apart: 4, of which 0 were waited for; matrix products, arithmetic and copies ran while one was open for 9% of the time, Pallas kernels for 0%

commit v1 on v0

--- a/solution.py
+++ b/solution.py
@@ -151,58 +151,6 @@
     )(value)
 
 
-def small_kernel(x_ref, o_ref, in_c, acc, in_1, in_2, in_3, send, recv):
-    z, y, c, x = position()
-    near = x * (1 - c) + y * c
-    nxt = y * (1 - c) + x * c
-    half = x_ref.shape[0] // 2
-    meet()
-    copy = remote(x_ref.at[rows((1 - c) * half, half)], in_c, send.at[0], recv.at[0], partner())
-    copy.start()
-    copy.wait()
-    value = x_ref[rows(c * half, half), :] + in_c[...]
-    stages = ((in_1, near, peer_near, 1), (in_2, nxt, peer_next, 4), (in_3, z, peer_far, 7))
-    for stage, (into, me, peers, first) in enumerate(stages):
-        acc[stage] = value
-        copies = []
-        for d in (1, 2, 3):
-            k = first + d - 1
-            copies.append(remote(acc.at[stage], into.at[me], send.at[k], recv.at[k], peers(d)))
-            copies[-1].start()
-        into[me] = value
-        for copy in copies:
-            copy.wait()
-        value = (into[0] + into[1]) + (into[2] + into[3])
-    block = o_ref.at[rows(c * half, half)]
-    o_ref[rows(c * half, half), :] = value
-    copy = remote(block, block, send.at[10], recv.at[10], partner())
-    copy.start()
-    copy.wait()
-
-
-def total_small(value):
-    n, w = value.shape
-    f = jnp.float32
-    vm = pl.BlockSpec(memory_space=pltpu.VMEM)
-    return pl.pallas_call(
-        small_kernel,
-        out_shape=jax.ShapeDtypeStruct(value.shape, f),
-        in_specs=[vm],
-        out_specs=vm,
-        scratch_shapes=[
-            pltpu.VMEM((n // 2, w), f),
-            pltpu.VMEM((3, n // 2, w), f),
-            pltpu.VMEM((4, n // 2, w), f),
-            pltpu.VMEM((4, n // 2, w), f),
-            pltpu.VMEM((4, n // 2, w), f),
-            pltpu.SemaphoreType.DMA((11,)),
-            pltpu.SemaphoreType.DMA((11,)),
-        ],
-        compiler_params=pltpu.CompilerParams(collective_id=1, has_side_effects=True),
-        name="total_small",
-    )(value)
-
-
 def split(value):
     high = value.astype(jnp.bfloat16)
     return high, (value - high.astype(jnp.float32)).astype(jnp.bfloat16)
@@ -372,71 +320,267 @@
         name="bases",
     )(order, cross_gram, start_block)
 
-def padded_2(value, sides, width):
-    edges = {}
-    for axis, dim in sides:
-        count, length = (lax.axis_size(axis), value.shape[dim])
-        up = [(i, (i + 1) % count) for i in range(count - 1)]
-        last = lax.slice_in_dim(value, length - width, length, axis=dim)
-        initial = lax.slice_in_dim(value, 0, width, axis=dim)
-        edges[dim] = (
-            lax.ppermute(last, axis, up),
-            lax.ppermute(initial, axis, [(b, a) for a, b in up]),
+
+def ring_peer(stage, d):
+    z, y, c, x = position()
+    k = lax.rem(stage + c, 3)
+    on_x = (2 - k) * (1 - k) // 2
+    on_y = k * (2 - k)
+    on_z = k * (k - 1) // 2
+    return (
+        lax.rem(z + d * on_z, 4), lax.rem(y + d * on_y, 4), c, lax.rem(x + d * on_x, 4)
+    )
+
+
+def ring_place(stage):
+    z, y, c, x = position()
+    k = lax.rem(stage + c, 3)
+    return x * ((2 - k) * (1 - k) // 2) + y * (k * (2 - k)) + z * (k * (k - 1) // 2)
+
+
+def slab_peer(step):
+    z, y, c, x = position()
+    s = lax.rem((z * 4 + y) * 2 + c + step + 32, 32)
+    return (s // 8, lax.rem(s // 2, 4), lax.rem(s, 2), x)
+
+
+def sub_peer(step):
+    z, y, c, x = position()
+    return (z, y, c, lax.rem(x + step + 4, 4))
+
+
+def shifted(value, step, length):
+    rows_in = lax.broadcasted_iota(jnp.int32, value.shape, 0)
+    at = lax.rem(rows_in, length)
+    edge = 0 if step == 1 else length - 1
+    return jnp.where(at == edge, 0.0, pltpu.roll(value, step % value.shape[0], 0))
+
+
+def project_kernel(
+    o_hbm, c_hbm, right_ref, left_ref, d_ref, drive_ref, sense_ref,
+    state_ref, input_ref, output_ref,
+    o_buf, c_buf, ctrl, obs, low_z, high_z, low_y, high_y, parts, in_c, acc, in_s,
+    load, send, recv,
+):
+    planes, lines, points, width = ctrl.shape
+    area = lines * points
+    z, y, c, x = position()
+    slab = (z * 4 + y) * 2 + c
+    barrier = pltpu.get_barrier_semaphore()
+    for to in (
+        [partner(), slab_peer(2 * c - 1)]
+        + [ring_peer(s, d) for s in range(3) for d in (1, 2, 3)]
+    ):
+        pl.semaphore_signal(barrier, inc=1, device_id=to, device_id_type=MESH)
+    loads = {}
+    order = (0, planes - 1) + tuple(range(1, planes - 1))
+    for p in order:
+        loads[p] = pltpu.make_async_copy(c_hbm.at[p], c_buf.at[p], load.at[p])
+        loads[p].start()
+    for p in range(planes):
+        pltpu.make_async_copy(o_hbm.at[p], o_buf.at[p], load.at[planes + p]).start()
+    r_high, r_low = split(right_ref[...])
+    r_both = jnp.concatenate([r_high, r_low], axis=0)
+    l_high, l_low = split(left_ref[...])
+    l_both = jnp.concatenate([l_high, l_low], axis=0)
+
+    down = remote(ctrl.at[0], high_z, send.at[0], recv.at[0], slab_peer(-1))
+    up = remote(ctrl.at[planes - 1], low_z, send.at[1], recv.at[1], slab_peer(1))
+    back = remote(ctrl.at[:, 0], high_y, send.at[2], recv.at[2], sub_peer(-1))
+    ahead = remote(ctrl.at[:, lines - 1], low_y, send.at[3], recv.at[3], sub_peer(1))
+
+    for p in order:
+        loads[p].wait()
+        high, low = split(c_buf[p].reshape(area, c_buf.shape[-1]))
+        both = mul(high, r_both, (1, 1))
+        value = both[:, :width] + both[:, width:] + mul(low, r_high, (1, 1))
+        ctrl[p] = value.reshape(lines, points, width)
+        if p == 0:
+            pl.semaphore_wait(barrier, 11)
+
+            @pl.when(slab > 0)
+            def _():
+                down.start()
+
+        if p == planes - 1:
+            @pl.when(slab < 31)
+            def _():
+                up.start()
+
+    @pl.when(x > 0)
+    def _():
+        back.start()
+
+    @pl.when(x < 3)
+    def _():
+        ahead.start()
+
+    @pl.when(slab == 0)
+    def _():
+        low_z[...] = jnp.zeros_like(low_z)
+
+    @pl.when(slab == 31)
+    def _():
+        high_z[...] = jnp.zeros_like(high_z)
+
+    @pl.when(x == 0)
+    def _():
+        low_y[...] = jnp.zeros_like(low_y)
+
+    @pl.when(x == 3)
+    def _():
+        high_y[...] = jnp.zeros_like(high_y)
+
+    parts[...] = jnp.zeros_like(parts)
+
+    def observe(p, _):
+        pltpu.make_async_copy(o_hbm.at[p], o_buf.at[p], load.at[planes + p]).wait()
+        high, low = split(o_buf[p].reshape(area, o_buf.shape[-1]))
+        both = mul(l_both, high, (1, 1))
+        value = both[:width] + both[width:] + mul(l_high, low, (1, 1))
+        v_high, v_low = split(value)
+        b_high, b_low = split(drive_ref[:, p, :])
+        count = drive_ref.shape[0]
+        parts[width : width + count, :] += (
+            mul(b_high, v_high, (1, 1)) + mul(b_low, v_high, (1, 1)) + mul(b_high, v_low, (1, 1))
         )
-    done = []
-    for _, dim in sides:
-        low, high = edges[dim]
-        around = [(width, width) if d in done else (0, 0) for d in range(value.ndim)]
-        value = jnp.concatenate([jnp.pad(low, around), value, jnp.pad(high, around)], axis=dim)
-        done.append(dim)
-    return value
-
-
-def matmul(first, second, contract):
-    return lax.dot_general(
-        first, second, (((contract[0],), (contract[1],)), ((), ())),
-        precision=lax.Precision.HIGH, preferred_element_type=jnp.float32,
-    )
-
-
-def stencil_padded(padded, conduct):
-    center = padded[1:-1, 1:-1]
-    beside = padded[2:, 1:-1] + padded[:-2, 1:-1] + padded[1:-1, 2:] + padded[1:-1, :-2]
-    along = jnp.pad(center, ((0, 0), (0, 0), (1, 1), (0, 0)))
-    beside = beside + along[:, :, 2:] + along[:, :, :-2]
-    return conduct[..., None] * (beside - 6.0 * center) / 6.0
-
+        obs[p] = value * (d_ref[pl.ds(p, 1), :] / 6.0)
+        return 0
+
+    lax.fori_loop(0, planes, observe, 0)
+
+    def spread(p):
+        center = ctrl[p]
+        below = low_z[...] if p == 0 else ctrl[p - 1]
+        above = high_z[...] if p == planes - 1 else ctrl[p + 1]
+        before = jnp.concatenate([low_y[p][None], ctrl[p, : lines - 1]], axis=0)
+        after = jnp.concatenate([ctrl[p, 1:], high_y[p][None]], axis=0)
+        flat = center.reshape(area, width)
+        rest = (below + above + before + after).reshape(area, width)
+        rest = rest + shifted(flat, 1, points) + shifted(flat, -1, points) - 6.0 * flat
+        x_high, x_low = split(rest)
+        f_high, f_low = split(flat)
+        w_high = jnp.concatenate([x_high, f_high], axis=1)
+        w_low = jnp.concatenate([x_low, f_low], axis=1)
+        count = sense_ref.shape[0]
+        ahead_rows = jnp.concatenate(
+            [obs[p], sense_ref[:, p, :], jnp.zeros((8 - count, area), jnp.float32)], axis=0
+        )
+        a_high, a_low = split(ahead_rows)
+        full = mul(a_high, w_high, (1, 0)) + mul(a_low, w_high, (1, 0)) + mul(a_high, w_low, (1, 0))
+        parts[:width, :] += full[:width, :width]
+        parts[width + 4 : width + 4 + count, :] += full[width : width + count, width:]
+
+    @pl.when(x > 0)
+    def _():
+        back.wait_send()
+        ahead.wait_recv()
+
+    @pl.when(x < 3)
+    def _():
+        ahead.wait_send()
+        back.wait_recv()
+
+    for p in range(1, planes - 1):
+        spread(p)
+
+    @pl.when(slab > 0)
+    def _():
+        down.wait_send()
+        up.wait_recv()
+
+    @pl.when(slab < 31)
+    def _():
+        up.wait_send()
+        down.wait_recv()
+
+    spread(0)
+    spread(planes - 1)
+
+    half = parts.shape[0] // 2
+    copy = remote(parts.at[rows((1 - c) * half, half)], in_c, send.at[4], recv.at[4], partner())
+    copy.start()
+    copy.wait()
+    value = parts[rows(c * half, half), :] + in_c[...]
+    for stage in range(3):
+        me = ring_place(stage)
+        acc[stage] = value
+        copies = []
+        for d in (1, 2, 3):
+            k = 4 + 3 * stage + d
+            copies.append(
+                remote(
+                    acc.at[stage], in_s.at[stage, me], send.at[k], recv.at[k], ring_peer(stage, d)
+                )
+            )
+            copies[-1].start()
+        in_s[stage, me] = value
+        for copy in copies:
+            copy.wait()
+        value = (in_s[stage, 0] + in_s[stage, 1]) + (in_s[stage, 2] + in_s[stage, 3])
+    acc[3] = value
+    copy = remote(acc.at[3], in_s.at[3, c], send.at[14], recv.at[14], partner())
+    copy.start()
+    in_s[3, c] = value
+    copy.wait()
+    whole = jnp.concatenate([in_s[3, 0], in_s[3, 1]], axis=0)
+    state_ref[...] = whole[:width]
+    ends = whole[width : width + 8]
+    input_ref[...] = ends.T[:, : input_ref.shape[1]]
+    output_ref[...] = ends[4 : 4 + output_ref.shape[0]]
+
+
+def project(observe, control, right, left, conduct, drive, sense):
+    planes, lines, points, rank = control.shape
+    n = right.shape[0]
+    area = lines * points
+    f = jnp.float32
+    vm = pl.BlockSpec(memory_space=pltpu.VMEM)
+    hbm = pl.BlockSpec(memory_space=pl.ANY)
+    size = n + 16
+    return pl.pallas_call(
+        project_kernel,
+        out_shape=(
+            jax.ShapeDtypeStruct((n, n), f),
+            jax.ShapeDtypeStruct((n, drive.shape[0]), f),
+            jax.ShapeDtypeStruct((sense.shape[0], n), f),
+        ),
+        in_specs=[hbm, hbm, vm, vm, vm, vm, vm],
+        out_specs=(vm, vm, vm),
+        scratch_shapes=[
+            pltpu.VMEM((planes, lines, points, rank), f),
+            pltpu.VMEM((planes, lines, points, rank), f),
+            pltpu.VMEM((planes, lines, points, n), f),
+            pltpu.VMEM((planes, n, area), f),
+            pltpu.VMEM((lines, points, n), f),
+            pltpu.VMEM((lines, points, n), f),
+            pltpu.VMEM((planes, points, n), f),
+            pltpu.VMEM((planes, points, n), f),
+            pltpu.VMEM((size, n), f),
+            pltpu.VMEM((size // 2, n), f),
+            pltpu.VMEM((4, size // 2, n), f),
+            pltpu.VMEM((4, 4, size // 2, n), f),
+            pltpu.SemaphoreType.DMA((2 * planes,)),
+            pltpu.SemaphoreType.DMA((15,)),
+            pltpu.SemaphoreType.DMA((15,)),
+        ],
+        compiler_params=pltpu.CompilerParams(
+            collective_id=1, has_side_effects=True, vmem_limit_bytes=60 * 1024 * 1024
+        ),
+        name="project",
+    )(observe, control, right, left, conduct, drive, sense)
 
 def on_device(factor_obs, factor_ctrl, diffusivity, input_map, output_map, start_block, order):
-    plane_count, line_count, point_count, rank_count = factor_ctrl.shape
-    cell_count = plane_count * line_count * point_count
-    observe = factor_obs.reshape(cell_count, rank_count)
-    control = factor_ctrl.reshape(cell_count, rank_count)
-    conduct = diffusivity.reshape(plane_count, line_count, point_count)
-    drive = input_map.reshape(input_map.shape[0], cell_count)
-    sense = output_map.reshape(output_map.shape[0], cell_count)
-    basis_count = start_block.shape[1]
-    cross_gram = total_big(gram(observe, control))
+    planes, lines, points, rank = factor_ctrl.shape
+    cells = planes * lines * points
+    cross_gram = total_big(
+        gram(factor_obs.reshape(cells, rank), factor_ctrl.reshape(cells, rank))
+    )
     right, left, reduced_mass = bases(cross_gram, start_block, order)
-    ctrl_space = matmul(control, right, (1, 1))
-    padded = padded_2(
-        ctrl_space.reshape(plane_count, line_count, point_count, basis_count),
-        ((SLAB, 0), ("sub", 1)),
-        1,
-    )
-    obs_space = matmul(observe, left, (1, 1))
-    applied = stencil_padded(padded, conduct).reshape(cell_count, basis_count)
-    parts = jnp.concatenate(
-        [
-            matmul(obs_space, applied, (0, 0)),
-            matmul(drive, obs_space, (1, 0)),
-            matmul(sense, ctrl_space, (1, 0)),
-            jnp.zeros((8, basis_count), jnp.float32),
-        ]
-    )
-    whole = total_small(parts)
-    n = basis_count
-    return (reduced_mass, whole[:n], whole[n : n + 4].T, whole[n + 4 : n + 8])
+    state, inputs, outputs = project(
+        factor_obs, factor_ctrl, right, left, diffusivity, input_map, output_map
+    )
+    return (reduced_mass, state, inputs, outputs)
 
 
 def solution(mesh):

time: 128 us -> 97.2 us (0.76)
  matrix products: 18.5 us -> 0 us
  starting transfers between devices: 8.57 us -> 0 us
  Pallas kernels: 84.8 us -> 91.4 us
  local copies, waits for them, and re-layouts: 9.25 us -> 4.19 us
  other arithmetic: 4.45 us -> 0 us
    dot_general x5 -> x0, matrix products: 18.5 us -> none  [matmul(): lax.dot_general(first, second, (((contract[0],), (contract[1],)), ((), ()...]
    ppermute x4 -> x0, starting transfers between devices: 8.57 us -> none  [the longest x2 4.96 us: padded_2(): lax.ppermute(last, axis, up)]
    pallas_call x1, Pallas kernels: 23.2 us -> 29.9 us  [project(): pl.pallas_call(project_kernel, out_shape=(jax.ShapeDtypeStruct((n, n), f)...]
    slice x6 -> x0, local copies, waits for them, and re-layouts: 5.8 us -> none  [the longest x2 2.81 us: on_device(): return (reduced_mass, whole[:n], whole[n:n + 4].T, whole[n + 4:n + 8])]
    div x1 -> x0, other arithmetic: 3.73 us -> none  [stencil_padded(): return conduct[..., None] * (beside - 6.0 * center) / 6.0]
    unnamed x14 -> x3, local copies, waits for them, and re-layouts: 1.44 us -> 4.19 us
    dot_general x1 -> x0, local copies, waits for them, and re-layouts: 1.84 us -> none  [matmul(): lax.dot_general(first, second, (((contract[0],), (contract[1],)), ((), ()...]
  transfers between devices with their start and end apart: 4 -> 0, of which waited for: 0 -> 0; matrix products, arithmetic and copies ran while one was open for 9% -> 0% of each run, Pallas kernels for 0% -> 0%
where the time goes in v1:
time: 97.2 us; the launch traced here: 96.8 us
  Pallas kernels  91.4 us (94%)
  local copies, waits for them, and re-layouts  4.19 us (4%)
  between operations  1.3 us (1%)
    pallas_call x1, Pallas kernels, total_big(): pl.pallas_call(big_kernel, out_shape=jax.ShapeDtypeStruct(value.shape, f)...  37.5 us
    pallas_call x1, Pallas kernels, project(): pl.pallas_call(project_kernel, out_shape=(jax.ShapeDtypeStruct((n, n), f)...  29.9 us
    pallas_call x1, Pallas kernels, bases(): pl.pallas_call(bases_kernel, out_shape=(jax.ShapeDtypeStruct((n, rank), f...  12.8 us
    pallas_call x1, Pallas kernels, gram(): pl.pallas_call(gram_kernel, grid=(cells // block,), out_shape=jax.ShapeDt...  11.2 us
    unnamed x3, local copies, waits for them, and re-layouts  4.19 us

profile of v1, /device:TPU:1, one launch (start us, length us, event | category | flops | bytes accessed | tf_op | source)
XLA Modules:
  0.0 96.8 jit_solution(13411115775733667067)
XLA Ops:
  0.6 11.2 %gram.1.x_ref = f32[512,512]{1,0:T(8,128)} custom-call(f32[4096,512]{1,0:T(8,128)} %bitcast.2, f32[4096,512]{1,0:T(8,128)} %bitcast.3), custom_call_target="tpu_custom_call" | custom-call | tf_op jit(solution)/shard_map/gram/pallas_call | solution.py:181
  11.8 37.5 %total_big.1.m_ref = f32[512,512]{1,0:T(8,128)} custom-call(f32[512,512]{1,0:T(8,128)} %gram.1.x_ref), custom_call_target="tpu_custom_call" | custom-call | tf_op jit(solution)/shard_map/total_big/pallas_call | solution.py:133
  50.0 12.8 %bases.1 = (f32[128,512]{1,0:T(8,128)}, f32[128,512]{1,0:T(8,128)}, f32[128,128]{1,0:T(8,128)}) custom-call(s32[1]{0:T(128)S(6)} %copy.14.order_ref, f32[512,512]{1,0:T(8,128)} %total_big.1.m_ref, f32[512,128]{1,0:T(8,128)} %s_ref.1), custom_call_target="tpu_custom_call" | custom-call | tf_op jit(solution)/shard_map/bases/pallas_call | solution.py:310
  62.8 29.9 %project.1 = (f32[128,128]{1,0:T(8,128)}, f32[128,4]{1,0:T(8,128)}, f32[4,128]{1,0:T(4,128)}) custom-call(f32[4,16,64,512]{3,2,1,0:T(8,128)} %o_hbm.1, f32[4,16,64,512]{3,2,1,0:T(8,128)} %c_hbm.1, f32[128,512]{1,0:T(8,128)} %get-tuple-element.11.right_ref, f32[128,512]{1,0:T(8,128)} %get-tuple-element.12.left_ref, f32[4,1024]{1,0:T(4,128)} %d_ref.1, ...), custom_call_target="tpu_custom_call" | custom-call | tf_op jit(solution)/shard_map/project/pallas_call | solution.py:541
  92.6 1.5 %copy.11 = f32[128,4]{0,1:T(4,128)} copy(f32[128,4]{1,0:T(8,128)} %get-tuple-element.18) | data formatting | bytes 4096
  94.1 1.5 %copy.15 = f32[128,128]{1,0:T(8,128)} copy(f32[128,128]{1,0:T(8,128)} %get-tuple-element.25) | data formatting | bytes 131072
  95.6 1.2 %copy.16 = f32[4,128]{1,0:T(4,128)} copy(f32[4,128]{1,0:T(4,128)} %get-tuple-element.27) | data formatting | bytes 4096

commit v2 on v1

--- a/solution.py
+++ b/solution.py
@@ -7,30 +7,34 @@
 from jax.sharding import PartitionSpec as P
 
 SLAB = ("slab_0", "slab_1", "slab_2")
+STEP = 16
+FLOOR = 1e-2
 
 MESH = pl.DeviceIdType.MESH
-STEP = 16
-FLOOR = 2e-4
 
 
 def position():
-    z, y, c, x = (lax.axis_index(n) for n in ("slab_0", "slab_1", "slab_2", "sub"))
-    return z, y, c, x
-
-
-def peer_near(d):
+    return tuple(lax.axis_index(n) for n in ("slab_0", "slab_1", "slab_2", "sub"))
+
+
+def axis_of(stage):
+    c = position()[2]
+    k = lax.rem(stage + c, 3)
+    return (2 - k) * (1 - k) // 2, k * (2 - k), k * (k - 1) // 2
+
+
+def ring_peer(stage, d):
     z, y, c, x = position()
-    return (z, lax.rem(y + d * c, 4), c, lax.rem(x + d * (1 - c), 4))
-
-
-def peer_next(d):
+    on_x, on_y, on_z = axis_of(stage)
+    return (
+        lax.rem(z + d * on_z, 4), lax.rem(y + d * on_y, 4), c, lax.rem(x + d * on_x, 4)
+    )
+
+
+def ring_place(stage):
     z, y, c, x = position()
-    return (z, lax.rem(y + d * (1 - c), 4), c, lax.rem(x + d * c, 4))
-
-
-def peer_far(d):
-    z, y, c, x = position()
-    return (lax.rem(z + d, 4), y, c, x)
+    on_x, on_y, on_z = axis_of(stage)
+    return x * on_x + y * on_y + z * on_z
 
 
 def partner():
@@ -38,15 +42,6 @@
     return (z, y, 1 - c, x)
 
 
-def meet():
-    barrier = pltpu.get_barrier_semaphore()
-    pl.semaphore_signal(barrier, inc=1, device_id=partner(), device_id_type=MESH)
-    for peers in (peer_near, peer_next, peer_far):
-        for d in (1, 2, 3):
-            pl.semaphore_signal(barrier, inc=1, device_id=peers(d), device_id_type=MESH)
-    pl.semaphore_wait(barrier, 10)
-
-
 def remote(src, dst, send, recv, to):
     return pltpu.make_async_remote_copy(
         src_ref=src, dst_ref=dst, send_sem=send, recv_sem=recv, device_id=to, device_id_type=MESH
@@ -55,100 +50,6 @@
 
 def rows(start, count):
     return pl.ds(pl.multiple_of(start, 8), count)
-
-
-def big_kernel(x_ref, o_ref, in_c, acc_c, in_1, acc_1, in_2, acc_2, in_z, send, recv):
-    z, y, c, x = position()
-    near = x * (1 - c) + y * c
-    nxt = y * (1 - c) + x * c
-    half = x_ref.shape[0] // 2
-    quarter = half // 4
-    piece = quarter // 4
-    meet()
-    copy = remote(x_ref.at[rows((1 - c) * half, half)], in_c, send.at[0], recv.at[0], partner())
-    copy.start()
-    copy.wait()
-    acc_c[...] = x_ref[rows(c * half, half), :] + in_c[...]
-    copies = []
-    for d in (1, 2, 3):
-        copies.append(
-            remote(
-                acc_c.at[rows(lax.rem(near + d, 4) * quarter, quarter)],
-                in_1.at[d - 1], send.at[d], recv.at[d], peer_near(d),
-            )
-        )
-        copies[-1].start()
-    for copy in copies:
-        copy.wait()
-    acc_1[...] = (acc_c[rows(near * quarter, quarter), :] + in_1[0]) + (in_1[1] + in_1[2])
-    copies = []
-    for d in (1, 2, 3):
-        copies.append(
-            remote(
-                acc_1.at[rows(lax.rem(nxt + d, 4) * piece, piece)],
-                in_2.at[d - 1], send.at[3 + d], recv.at[3 + d], peer_next(d),
-            )
-        )
-        copies[-1].start()
-    for copy in copies:
-        copy.wait()
-    mine = (acc_1[rows(nxt * piece, piece), :] + in_2[0]) + (in_2[1] + in_2[2])
-    acc_2[...] = mine
-    copies = []
-    for d in (1, 2, 3):
-        copies.append(
-            remote(acc_2, in_z.at[z], send.at[6 + d], recv.at[6 + d], peer_far(d))
-        )
-        copies[-1].start()
-    in_z[z] = mine
-    for copy in copies:
-        copy.wait()
-    low = c * half + near * quarter
-    at = low + nxt * piece
-    o_ref[rows(at, piece), :] = (in_z[0] + in_z[1]) + (in_z[2] + in_z[3])
-    copies = []
-    for d in (1, 2, 3):
-        block = o_ref.at[rows(at, piece)]
-        copies.append(remote(block, block, send.at[9 + d], recv.at[9 + d], peer_next(d)))
-        copies[-1].start()
-    for copy in copies:
-        copy.wait()
-    copies = []
-    for d in (1, 2, 3):
-        block = o_ref.at[rows(low, quarter)]
-        copies.append(remote(block, block, send.at[12 + d], recv.at[12 + d], peer_near(d)))
-        copies[-1].start()
-    for copy in copies:
-        copy.wait()
-    block = o_ref.at[rows(c * half, half)]
-    copy = remote(block, block, send.at[16], recv.at[16], partner())
-    copy.start()
-    copy.wait()
-
-
-def total_big(value):
-    n, w = value.shape
-    f = jnp.float32
-    vm = pl.BlockSpec(memory_space=pltpu.VMEM)
-    return pl.pallas_call(
-        big_kernel,
-        out_shape=jax.ShapeDtypeStruct(value.shape, f),
-        in_specs=[vm],
-        out_specs=vm,
-        scratch_shapes=[
-            pltpu.VMEM((n // 2, w), f),
-            pltpu.VMEM((n // 2, w), f),
-            pltpu.VMEM((3, n // 8, w), f),
-            pltpu.VMEM((n // 8, w), f),
-            pltpu.VMEM((3, n // 32, w), f),
-            pltpu.VMEM((n // 32, w), f),
-            pltpu.VMEM((4, n // 32, w), f),
-            pltpu.SemaphoreType.DMA((17,)),
-            pltpu.SemaphoreType.DMA((17,)),
-        ],
-        compiler_params=pltpu.CompilerParams(collective_id=0, has_side_effects=True),
-        name="total_big",
-    )(value)
 
 
 def split(value):
@@ -163,36 +64,195 @@
     )
 
 
-def gram_kernel(o_ref, c_ref, out_ref):
-    @pl.when(pl.program_id(0) == 0)
-    def _():
-        out_ref[...] = jnp.zeros_like(out_ref)
-
-    o_high, o_low = split(o_ref[...])
-    c_high, c_low = split(c_ref[...])
-    out_ref[...] += (
-        mul(o_high, c_high, (0, 0)) + mul(o_high, c_low, (0, 0)) + mul(o_low, c_high, (0, 0))
-    )
-
-
-def gram(observe, control, block=1024):
+def cross_kernel(
+    o_hbm, c_hbm, out_ref,
+    o_buf, c_buf, c_high, c_low, turned, away, own, in_c, acc_c, in_1, acc_1, in_2, acc_2, in_3,
+    load, send, recv,
+):
+    chunks = o_buf.shape[0]
+    rank = c_buf.shape[-1]
+    half = rank // 2
+    quarter = half // 4
+    piece = quarter // 4
+    z, y, c, x = position()
+    barrier = pltpu.get_barrier_semaphore()
+    for to in [partner()] + [ring_peer(s, d) for s in range(3) for d in (1, 2, 3)]:
+        pl.semaphore_signal(barrier, inc=1, device_id=to, device_id_type=MESH)
+    loads = []
+    for k in range(chunks):
+        for j, (src, dst) in enumerate(((c_hbm, c_buf), (o_hbm, o_buf))):
+            loads.append(pltpu.make_async_copy(src.at[k], dst.at[k], load.at[2 * k + j]))
+            loads[-1].start()
+
+    def columns(which):
+        return pl.ds(pl.multiple_of(which * half, half), half)
+
+    def thrice(both, high, low):
+        full = mul(both, high, (1, 0))
+        return full[:half] + full[half:] + mul(both[:half], low, (1, 0))
+
+    def turn(value):
+        high, low = split(value.T)
+        return jnp.concatenate([high, low], axis=0)
+
+    for k in range(chunks):
+        loads[2 * k].wait()
+        high, low = split(c_buf[k])
+        c_high[k] = high
+        c_low[k] = low
+        loads[2 * k + 1].wait()
+        term = thrice(turn(o_buf[k, :, columns(1 - c)]), high, low)
+        away[...] = term if k == 0 else away[...] + term
+    pl.semaphore_wait(barrier, 10)
+    across = remote(away, in_c, send.at[0], recv.at[0], partner())
+    across.start()
+
+    first = ring_place(0)
+    second = ring_place(1)
+    third = ring_place(2)
+    low_row = c * half + first * quarter
+    at_row = low_row + second * piece
+
+    def three(start, make):
+        copies = []
+        for d in (1, 2, 3):
+            copies.append(make(d, send.at[start + d], recv.at[start + d]))
+            copies[-1].start()
+        return copies
+
+    def done(copies):
+        for copy in copies:
+            copy.wait()
+
+    def reduce_1(p):
+        return three(3 * p, lambda d, s, r: remote(
+            acc_c.at[p, rows(lax.rem(first + d, 4) * quarter, quarter)],
+            in_1.at[p, d - 1], s, r, ring_peer(0, d)))
+
+    def reduce_2(p):
+        acc_1[p] = (acc_c[p, rows(first * quarter, quarter), :] + in_1[p, 0]) + (
+            in_1[p, 1] + in_1[p, 2]
+        )
+        return three(6 + 3 * p, lambda d, s, r: remote(
+            acc_1.at[p, rows(lax.rem(second + d, 4) * piece, piece)],
+            in_2.at[p, d - 1], s, r, ring_peer(1, d)))
+
+    def reduce_3(p):
+        mine = (acc_1[p, rows(second * piece, piece), :] + in_2[p, 0]) + (in_2[p, 1] + in_2[p, 2])
+        acc_2[p] = mine
+        copies = three(12 + 3 * p, lambda d, s, r: remote(
+            acc_2.at[p], in_3.at[p, third], s, r, ring_peer(2, d)))
+        in_3[p, third] = mine
+        return copies
+
+    def gather_2(p):
+        block = out_ref.at[rows(at_row, piece), p * half : (p + 1) * half]
+        out_ref[rows(at_row, piece), p * half : (p + 1) * half] = (in_3[p, 0] + in_3[p, 1]) + (
+            in_3[p, 2] + in_3[p, 3]
+        )
+        return three(18 + 3 * p, lambda d, s, r: remote(block, block, s, r, ring_peer(1, d)))
+
+    def gather_1(p):
+        block = out_ref.at[rows(low_row, quarter), p * half : (p + 1) * half]
+        copies = three(24 + 3 * p, lambda d, s, r: remote(block, block, s, r, ring_peer(0, d)))
+        copies.append(remote(block, block, send.at[31 + 4 * p], recv.at[31 + 4 * p], partner()))
+        copies[-1].start()
+        return copies
+
+    def forward(p, copies):
+        passed = [copies[3]]
+        for d in (1, 2, 3):
+            copies[d - 1].wait_recv()
+            row = c * half + lax.rem(first + 4 - d, 4) * quarter
+            block = out_ref.at[rows(row, quarter), p * half : (p + 1) * half]
+            k = 31 + 4 * p + d
+            passed.append(remote(block, block, send.at[k], recv.at[k], partner()))
+            passed[-1].start()
+        return passed
+
+    for k in range(chunks):
+        both = turn(o_buf[k, :, columns(c)])
+        turned[k] = both
+        term = thrice(both, c_high[k, :, :half], c_low[k, :, :half])
+        own[...] = term if k == 0 else own[...] + term
+    across.wait()
+    acc_c[0] = own[...] + in_c[:, :half]
+    moving_0 = reduce_1(0)
+    for k in range(chunks):
+        term = thrice(turned[k], c_high[k, :, half:], c_low[k, :, half:])
+        own[...] = term if k == 0 else own[...] + term
+    acc_c[1] = own[...] + in_c[:, half:]
+    moving_1 = reduce_1(1)
+    for stage in (reduce_2, reduce_3, gather_2, gather_1):
+        done(moving_0)
+        moving_0 = stage(0)
+        done(moving_1)
+        moving_1 = stage(1)
+    passed_0 = forward(0, moving_0)
+    passed_1 = forward(1, moving_1)
+    for copies, passed in ((moving_0, passed_0), (moving_1, passed_1)):
+        for copy in copies[:3]:
+            copy.wait_send()
+        done(passed)
+
+
+def cross(observe, control, chunks=4):
     cells, rank = observe.shape
-    spec = pl.BlockSpec((block, rank), lambda k: (k, 0))
+    f = jnp.float32
+    b = jnp.bfloat16
+    depth = cells // chunks
+    half = rank // 2
+    hbm = pl.BlockSpec(memory_space=pltpu.HBM)
     return pl.pallas_call(
-        gram_kernel,
-        grid=(cells // block,),
-        out_shape=jax.ShapeDtypeStruct((rank, rank), jnp.float32),
-        in_specs=[spec, spec],
-        out_specs=pl.BlockSpec((rank, rank), lambda k: (0, 0)),
-        compiler_params=pltpu.CompilerParams(dimension_semantics=("arbitrary",)),
-        name="gram",
-    )(observe, control)
+        cross_kernel,
+        out_shape=jax.ShapeDtypeStruct((rank, rank), f),
+        in_specs=[hbm, hbm],
+        out_specs=pl.BlockSpec(memory_space=pltpu.VMEM),
+        scratch_shapes=[
+            pltpu.VMEM((chunks, depth, rank), f),
+            pltpu.VMEM((chunks, depth, rank), f),
+            pltpu.VMEM((chunks, depth, rank), b),
+            pltpu.VMEM((chunks, depth, rank), b),
+            pltpu.VMEM((chunks, rank, depth), b),
+            pltpu.VMEM((half, rank), f),
+            pltpu.VMEM((half, half), f),
+            pltpu.VMEM((half, rank), f),
+            pltpu.VMEM((2, half, half), f),
+            pltpu.VMEM((2, 3, half // 4, half), f),
+            pltpu.VMEM((2, half // 4, half), f),
+            pltpu.VMEM((2, 3, half // 16, half), f),
+            pltpu.VMEM((2, half // 16, half), f),
+            pltpu.VMEM((2, 4, half // 16, half), f),
+            pltpu.SemaphoreType.DMA((2 * chunks,)),
+            pltpu.SemaphoreType.DMA((39,)),
+            pltpu.SemaphoreType.DMA((39,)),
+        ],
+        compiler_params=pltpu.CompilerParams(
+            collective_id=0, has_side_effects=True, vmem_limit_bytes=50 * 1024 * 1024
+        ),
+        name="cross",
+    )(observe.reshape(chunks, depth, rank), control.reshape(chunks, depth, rank))
 
 
 def product(first, second, contract):
     return lax.dot_general(
         first, second, (((contract[0],), (contract[1],)), ((), ())),
         precision=lax.Precision.HIGHEST, preferred_element_type=jnp.float32,
+    )
+
+
+def narrow(first, second):
+    f1 = first.astype(jnp.bfloat16).astype(jnp.float32)
+    f2 = (first - f1).astype(jnp.bfloat16).astype(jnp.float32)
+    f3 = first - f1 - f2
+    s1 = second.astype(jnp.bfloat16).astype(jnp.float32)
+    s2 = (second - s1).astype(jnp.bfloat16).astype(jnp.float32)
+    s3 = second - s1 - s2
+    a = jnp.concatenate([f1, f1, f2, f1, f2, f3], axis=0).T
+    b = jnp.concatenate([s1, s2, s1, s3, s2, s1], axis=0)
+    return lax.dot_general(
+        a.astype(jnp.bfloat16), b.astype(jnp.bfloat16), (((1,), (0,)), ((), ())),
+        preferred_element_type=jnp.float32,
     )
 
 
@@ -247,23 +307,31 @@
             b[here, :] = lower
             if first + STEP < n:
                 rest = slice(first + STEP, n)
-                change = product(upper, jnp.concatenate([upper, lower], axis=1), (0, 0))
+                change = narrow(upper, jnp.concatenate([upper, lower], axis=1))
                 a[rest, :] = a[rest, :] - change[rest, :n]
                 b[rest, :] = b[rest, :] - change[rest, n:]
     return least
 
 
+def by_halves(first, high, low, contract):
+    n = first.shape[0]
+    f_high, f_low = split(first)
+    both = mul(jnp.concatenate([f_high, f_low], axis=0), high, contract)
+    return both[:n] + both[n:] + mul(f_high, low, contract)
+
+
 def unit_rows(value):
     return value * lax.rsqrt(jnp.sum(value * value, axis=1, keepdims=True))
 
 
-def bases_kernel(order_ref, m_ref, s_ref, right_ref, left_ref, mass_ref, a3, b3, a4, b4, y3, y4):
+def bases_kernel(order_ref, m_ref, s_ref, right_ref, left_ref, mass_ref, a3, b3, a4, b4, y3, y4, high, low):
     n = a3.shape[0]
     m = m_ref
-    y1 = unit_rows(product(s_ref[...].T, m[...], (1, 0)))
-    y2 = unit_rows(product(y1, m[...], (1, 1)))
-    y3[...] = unit_rows(product(y2, m[...], (1, 0)))
-    y4[...] = product(y3[...], m[...], (1, 1))
+    high[...], low[...] = split(m[...])
+    y1 = unit_rows(by_halves(s_ref[...].T, high[...], low[...], (1, 0)))
+    y2 = unit_rows(by_halves(y1, high[...], low[...], (1, 1)))
+    y3[...] = unit_rows(by_halves(y2, high[...], low[...], (1, 0)))
+    y4[...] = by_halves(y3[...], high[...], low[...], (1, 1))
     a3[...] = product(y3[...], y3[...], (1, 1))
     a4[...] = product(y4[...], y4[...], (1, 1))
     least = factor(((a3, b3), (a4, b4)))
@@ -316,26 +384,14 @@
         ),
         in_specs=[pl.BlockSpec(memory_space=pltpu.SMEM), vm, vm],
         out_specs=(vm, vm, vm),
-        scratch_shapes=[pltpu.VMEM((n, n), f)] * 4 + [pltpu.VMEM((n, rank), f)] * 2,
+        scratch_shapes=[pltpu.VMEM((n, n), f)] * 4 + [pltpu.VMEM((n, rank), f)] * 2
+        + [pltpu.VMEM((rank, rank), jnp.bfloat16)] * 2,
+        compiler_params=pltpu.CompilerParams(vmem_limit_bytes=16 * 1024 * 1024),
+        cost_estimate=pl.CostEstimate(
+            flops=8 * 6 * 2 * n * rank * rank, bytes_accessed=4 * rank * rank, transcendentals=0
+        ),
         name="bases",
     )(order, cross_gram, start_block)
-
-
-def ring_peer(stage, d):
-    z, y, c, x = position()
-    k = lax.rem(stage + c, 3)
-    on_x = (2 - k) * (1 - k) // 2
-    on_y = k * (2 - k)
-    on_z = k * (k - 1) // 2
-    return (
-        lax.rem(z + d * on_z, 4), lax.rem(y + d * on_y, 4), c, lax.rem(x + d * on_x, 4)
-    )
-
-
-def ring_place(stage):
-    z, y, c, x = position()
-    k = lax.rem(stage + c, 3)
-    return x * ((2 - k) * (1 - k) // 2) + y * (k * (2 - k)) + z * (k * (k - 1) // 2)
 
 
 def slab_peer(step):
@@ -357,9 +413,9 @@
 
 
 def project_kernel(
-    o_hbm, c_hbm, right_ref, left_ref, d_ref, drive_ref, sense_ref,
-    state_ref, input_ref, output_ref,
-    o_buf, c_buf, ctrl, obs, low_z, high_z, low_y, high_y, parts, in_c, acc, in_s,
+    c_ref, o_hbm, right_ref, left_ref, d_ref, drive_ref, sense_ref,
+    out_ref,
+    o_buf, ctrl, obs, low_z, high_z, low_y, high_y, parts, in_c, acc, in_s,
     load, send, recv,
 ):
     planes, lines, points, width = ctrl.shape
@@ -372,13 +428,9 @@
         + [ring_peer(s, d) for s in range(3) for d in (1, 2, 3)]
     ):
         pl.semaphore_signal(barrier, inc=1, device_id=to, device_id_type=MESH)
-    loads = {}
     order = (0, planes - 1) + tuple(range(1, planes - 1))
-    for p in order:
-        loads[p] = pltpu.make_async_copy(c_hbm.at[p], c_buf.at[p], load.at[p])
-        loads[p].start()
     for p in range(planes):
-        pltpu.make_async_copy(o_hbm.at[p], o_buf.at[p], load.at[planes + p]).start()
+        pltpu.make_async_copy(o_hbm.at[p], o_buf.at[p], load.at[p]).start()
     r_high, r_low = split(right_ref[...])
     r_both = jnp.concatenate([r_high, r_low], axis=0)
     l_high, l_low = split(left_ref[...])
@@ -390,8 +442,7 @@
     ahead = remote(ctrl.at[:, lines - 1], low_y, send.at[3], recv.at[3], sub_peer(1))
 
     for p in order:
-        loads[p].wait()
-        high, low = split(c_buf[p].reshape(area, c_buf.shape[-1]))
+        high, low = split(c_ref[p].reshape(area, c_ref.shape[-1]))
         both = mul(high, r_both, (1, 1))
         value = both[:, :width] + both[:, width:] + mul(low, r_high, (1, 1))
         ctrl[p] = value.reshape(lines, points, width)
@@ -434,7 +485,7 @@
     parts[...] = jnp.zeros_like(parts)
 
     def observe(p, _):
-        pltpu.make_async_copy(o_hbm.at[p], o_buf.at[p], load.at[planes + p]).wait()
+        pltpu.make_async_copy(o_hbm.at[p], o_buf.at[p], load.at[p]).wait()
         high, low = split(o_buf[p].reshape(area, o_buf.shape[-1]))
         both = mul(l_both, high, (1, 1))
         value = both[:width] + both[width:] + mul(l_high, low, (1, 1))
@@ -523,11 +574,16 @@
     copy.start()
     in_s[3, c] = value
     copy.wait()
-    whole = jnp.concatenate([in_s[3, 0], in_s[3, 1]], axis=0)
-    state_ref[...] = whole[:width]
-    ends = whole[width : width + 8]
-    input_ref[...] = ends.T[:, : input_ref.shape[1]]
-    output_ref[...] = ends[4 : 4 + output_ref.shape[0]]
+    out_ref[:half, :] = in_s[3, 0]
+    out_ref[half:, :] = in_s[3, 1]
+
+
+def finish_kernel(whole_ref, state_ref, input_ref, output_ref):
+    n = state_ref.shape[0]
+    count = input_ref.shape[0]
+    state_ref[...] = whole_ref[:n, :]
+    input_ref[...] = whole_ref[n : n + count, :]
+    output_ref[...] = whole_ref[n + 4 : n + 4 + output_ref.shape[0], :]
 
 
 def project(observe, control, right, left, conduct, drive, sense):
@@ -536,19 +592,14 @@
     area = lines * points
     f = jnp.float32
     vm = pl.BlockSpec(memory_space=pltpu.VMEM)
-    hbm = pl.BlockSpec(memory_space=pl.ANY)
+    hbm = pl.BlockSpec(memory_space=pltpu.HBM)
     size = n + 16
-    return pl.pallas_call(
+    whole = pl.pallas_call(
         project_kernel,
-        out_shape=(
-            jax.ShapeDtypeStruct((n, n), f),
-            jax.ShapeDtypeStruct((n, drive.shape[0]), f),
-            jax.ShapeDtypeStruct((sense.shape[0], n), f),
-        ),
-        in_specs=[hbm, hbm, vm, vm, vm, vm, vm],
-        out_specs=(vm, vm, vm),
+        out_shape=jax.ShapeDtypeStruct((size, n), f),
+        in_specs=[vm, hbm] + [vm] * 5,
+        out_specs=vm,
         scratch_shapes=[
-            pltpu.VMEM((planes, lines, points, rank), f),
             pltpu.VMEM((planes, lines, points, rank), f),
             pltpu.VMEM((planes, lines, points, n), f),
             pltpu.VMEM((planes, n, area), f),
@@ -560,22 +611,33 @@
             pltpu.VMEM((size // 2, n), f),
             pltpu.VMEM((4, size // 2, n), f),
             pltpu.VMEM((4, 4, size // 2, n), f),
-            pltpu.SemaphoreType.DMA((2 * planes,)),
+            pltpu.SemaphoreType.DMA((planes,)),
             pltpu.SemaphoreType.DMA((15,)),
             pltpu.SemaphoreType.DMA((15,)),
         ],
         compiler_params=pltpu.CompilerParams(
-            collective_id=1, has_side_effects=True, vmem_limit_bytes=60 * 1024 * 1024
+            collective_id=1, has_side_effects=True, vmem_limit_bytes=42 * 1024 * 1024
         ),
         name="project",
-    )(observe, control, right, left, conduct, drive, sense)
+    )(control, observe, right, left, conduct, drive, sense)
+    state, inputs, outputs = pl.pallas_call(
+        finish_kernel,
+        out_shape=(
+            jax.ShapeDtypeStruct((n, n), f),
+            jax.ShapeDtypeStruct((drive.shape[0], n), f),
+            jax.ShapeDtypeStruct((sense.shape[0], n), f),
+        ),
+        in_specs=[vm],
+        out_specs=(vm, vm, vm),
+        compiler_params=pltpu.CompilerParams(vmem_limit_bytes=4 * 1024 * 1024),
+        name="finish",
+    )(whole)
+    return state, inputs.T, outputs
 
 def on_device(factor_obs, factor_ctrl, diffusivity, input_map, output_map, start_block, order):
     planes, lines, points, rank = factor_ctrl.shape
     cells = planes * lines * points
-    cross_gram = total_big(
-        gram(factor_obs.reshape(cells, rank), factor_ctrl.reshape(cells, rank))
-    )
+    cross_gram = cross(factor_obs.reshape(cells, rank), factor_ctrl.reshape(cells, rank))
     right, left, reduced_mass = bases(cross_gram, start_block, order)
     state, inputs, outputs = project(
         factor_obs, factor_ctrl, right, left, diffusivity, input_map, output_map

time: 97.2 us -> 81 us (0.83)
  Pallas kernels: 91.4 us -> 79.5 us
  local copies, waits for them, and re-layouts: 4.19 us -> 0.03 us
    pallas_call x3, Pallas kernels: 78.6 us -> 71.4 us  [the longest x1 43.5 us: cross(): pl.pallas_call(cross_kernel, out_shape=jax.ShapeDtypeStruct((rank, rank),...]
    pallas_call x1, Pallas kernels: 12.8 us -> 8.1 us  [bases(): pl.pallas_call(bases_kernel, out_shape=(jax.ShapeDtypeStruct((n, rank), f...]
    unnamed x3 -> x10, local copies, waits for them, and re-layouts: 4.19 us -> 0.03 us
where the time goes in v2:
time: 81 us; the launch traced here: 80.9 us
  Pallas kernels  79.5 us (98%)
  between operations  1.35 us (2%)
    pallas_call x1, Pallas kernels, cross(): pl.pallas_call(cross_kernel, out_shape=jax.ShapeDtypeStruct((rank, rank),...  43.5 us
    pallas_call x1, Pallas kernels, project(): pl.pallas_call(project_kernel, out_shape=jax.ShapeDtypeStruct((size, n),...  27.3 us
    pallas_call x1, Pallas kernels, bases(): pl.pallas_call(bases_kernel, out_shape=(jax.ShapeDtypeStruct((n, rank), f...  8.1 us

profile of v2, /device:TPU:1, one launch (start us, length us, event | category | flops | bytes accessed | tf_op | source)
XLA Modules:
  0.0 80.9 jit_solution(12739040227600851742)
XLA Ops:
  1.3 0.0 copy-start.4
  1.3 43.5 %cross.1.m_ref = f32[512,512]{1,0:T(8,128)S(1)} custom-call(f32[4,1024,512]{2,1,0:T(8,128)} %bitcast.4, f32[4,1024,512]{2,1,0:T(8,128)} %bitcast.3), custom_call_target="tpu_custom_call" | custom-call | tf_op jit(solution)/shard_map/cross/pallas_call | solution.py:206
  44.8 0.0 copy-done.4
  44.8 0.0 copy-start
  44.8 0.0 copy-start.1
  44.8 0.0 copy-start.2
  44.8 0.0 copy-start.3
  44.8 8.1 %bases.1 = (f32[128,512]{1,0:T(8,128)S(1)}, f32[128,512]{1,0:T(8,128)S(1)}, f32[128,128]{1,0:T(8,128)}) custom-call(s32[1]{0:T(128)S(6)} %copy.11.order_ref, f32[512,512]{1,0:T(8,128)S(1)} %cross.1.m_ref, f32[512,128]{1,0:T(8,128)S(1)} %copy-done.4), custom_call_target="tpu_custom_call" | custom-call | flops 3221225472 | bytes 1048576 | tf_op jit(solution)/shard_map/bases/pallas_call | solution.py:378
  52.9 0.0 copy-done
  52.9 0.0 copy-done.1
  52.9 0.0 copy-done.2
  52.9 0.0 copy-done.3
  52.9 27.3 %project.1.whole_ref = f32[144,128]{1,0:T(8,128)S(1)} custom-call(f32[4,16,64,512]{3,2,1,0:T(8,128)S(1)} %copy-done, f32[4,16,64,512]{3,2,1,0:T(8,128)} %o_hbm.1, f32[128,512]{1,0:T(8,128)S(1)} %get-tuple-element.11.right_ref, f32[128,512]{1,0:T(8,128)S(1)} %get-tuple-element.12.left_ref, f32[4,1024]{1,0:T(4,128)S(1)} %copy-done.3, ...), custom_call_target="tpu_custom_call" | custom-call | tf_op jit(solution)/shard_map/project/pallas_call | solution.py:597
  80.2 0.6 finish.1
Async XLA Ops:
  1.3 43.5 %copy-start.4 = (f32[512,128]{1,0:T(8,128)S(1)}, f32[512,128]{1,0:T(8,128)}, u32[]{:S(2)}) copy-start(f32[512,128]{1,0:T(8,128)} %s_ref.1) | copy-start | bytes 786436
  44.8 8.2 %copy-start = (f32[4,16,64,512]{3,2,1,0:T(8,128)S(1)}, f32[4,16,64,512]{3,2,1,0:T(8,128)}, u32[]{:S(2)}) copy-start(f32[4,16,64,512]{3,2,1,0:T(8,128)} %c_ref.1) | copy-start | bytes 25165828
  44.8 8.1 %copy-start.1 = (f32[4,4,1024]{2,1,0:T(4,128)S(1)}, f32[4,4,1024]{2,1,0:T(4,128)}, u32[]{:S(2)}) copy-start(f32[4,4,1024]{2,1,0:T(4,128)} %drive_ref.1) | copy-start | bytes 196612
  44.8 8.1 %copy-start.2 = (f32[4,4,1024]{2,1,0:T(4,128)S(1)}, f32[4,4,1024]{2,1,0:T(4,128)}, u32[]{:S(2)}) copy-start(f32[4,4,1024]{2,1,0:T(4,128)} %sense_ref.1) | copy-start | bytes 196612
  44.8 8.1 %copy-start.3 = (f32[4,1024]{1,0:T(4,128)S(1)}, f32[4,1024]{1,0:T(4,128)}, u32[]{:S(2)}) copy-start(f32[4,1024]{1,0:T(4,128)} %d_ref.1) | copy-start | bytes 49156
